TPU v7x, 128 devices: a whole 4x4x4 slice. The times are simulated.
128 devices in a mesh: grp: 8 (over z, y_lo), dev: 16 (over x, y_hi, core).
Axes of the slice: x: 4, y: 4 (y_hi: 2, y_lo: 2; y = y_hi * 2 + y_lo), z: 4, core: 2. Of those that a mesh axis runs over, the one named last changes fastest.
Arguments:
- vertex_values: bfloat16 [8192, 128, 256], P(('grp', 'dev')), may hold values from -6 to 6
- position_domain_label: int32 [8192], P(('grp', 'dev')), may hold values from 0 to 64, as said below
- position_vertex_tally: int32 [8192], P(('grp', 'dev')), may hold values from 0 to 128, as said below
- normalizer_gain: float32 [256], replicated, may hold values from 0.1 to 1.9
- embedding_matrix: bfloat16 [256, 256], replicated, may hold values from -0.375 to 0.375
- partition_input_matrix: bfloat16 [256, 256], replicated, may hold values from -0.375 to 0.375
- partition_score_matrix: bfloat16 [32, 64], replicated, may hold values from -60 to 60
- softmax_sharpness: float32 [8], replicated, may hold values from 0.3 to 1
- partition_attention_maps: float32 [3, 32, 32], replicated, may hold values from -10 to 10
- readout_matrix: bfloat16 [256, 256], replicated, may hold values from -1.5 to 1.5
Outputs:
- updated: bfloat16 [8192, 128, 256], P(('grp', 'dev'))
Inputs may be any that keep to these rules, and one draw needn't show every extreme that they name: `position_domain_label`: on each device the used slots come first; a device may use none. Reading the devices in order and their used slots in order lists every mesh's blocks as one run, meshes in increasing order, each mesh 2 or more blocks. Exactly 4096 slots are used in all, and some device uses all 64 of its slots. `position_vertex_tally`: 128 in every used slot except the last block of each mesh, which holds 1 to 128; 0 in unused slots.
All inputs are finite; a program needn't handle non-finite values.
Results may differ from a plain program's by a relative error of at most 0.012.
The roundings to bfloat16 on the way count: a program that leaves them out, or rounds other values in their place, can miss the bound.
Values may be sent and summed in bfloat16 or wider, within the bound.
No kernel may reach another device: no remote copies, remote signals or barrier semaphores. Data moves between devices by JAX's collectives and lax.ppermute only.
A program may use at most 128 MiB of HBM per device.

v0:
```python
import jax
import jax.numpy as jnp
from jax import lax
from jax.sharding import PartitionSpec as P

MESHES = 64


def partition_routine(
    tile_sequence,
    vertex_tallies,
    domain_sequence,
    normalizer_gain,
    embedding_matrix,
    partition_input_matrix,
    partition_score_matrix,
    softmax_sharpness,
):
    tile_amount, tile_height, model_width = tile_sequence.shape
    attention_group_amount = softmax_sharpness.shape[0]
    head_width = model_width // attention_group_amount
    partition_amount = partition_score_matrix.shape[1]
    flattened = tile_sequence.reshape(tile_amount * tile_height, model_width).astype(jnp.float32)
    centre = flattened - jnp.mean(flattened, axis=1, keepdims=True)
    spread = jnp.mean(centre * centre, axis=1, keepdims=True)
    normed = (centre * lax.rsqrt(spread + 1e-05) * normalizer_gain).astype(jnp.bfloat16)
    features = jnp.dot(normed, embedding_matrix, preferred_element_type=jnp.float32).astype(
        jnp.bfloat16
    )
    middles = jnp.dot(normed, partition_input_matrix, preferred_element_type=jnp.float32).astype(
        jnp.bfloat16
    )
    partition_scores = jnp.dot(
        middles.reshape(-1, head_width), partition_score_matrix, preferred_element_type=jnp.float32
    )
    partition_scores = (
        partition_scores.reshape(tile_amount, tile_height, attention_group_amount, partition_amount)
        / softmax_sharpness[:, None]
    )
    living = (
        lax.broadcasted_iota(jnp.int32, (tile_amount, tile_height), 1) < vertex_tallies[:, None]
    ).astype(jnp.float32)
    partition_shares = (
        jax.nn.softmax(partition_scores, axis=-1) * living[:, :, None, None]
    ).astype(jnp.bfloat16)
    partial_sums = jnp.einsum(
        "bphm,bphd->bhmd",
        partition_shares,
        features.reshape(tile_amount, tile_height, attention_group_amount, head_width),
        preferred_element_type=jnp.float32,
    )
    partial_totals = jnp.sum(partition_shares.astype(jnp.float32), axis=1)
    one_hot = (
        domain_sequence[:, None] == lax.broadcasted_iota(jnp.int32, (tile_amount, MESHES), 1)
    ).astype(jnp.float32)
    domain_accumulated = jnp.dot(one_hot.T, partial_sums.reshape(tile_amount, -1))
    domain_share_accumulated = jnp.dot(one_hot.T, partial_totals.reshape(tile_amount, -1))
    return (
        partition_shares.reshape(
            tile_amount, tile_height, attention_group_amount * partition_amount
        ),
        domain_accumulated,
        domain_share_accumulated,
    )


def attend_tokens(domain_accumulated, domain_share_accumulated, partition_attention_maps):
    row_count, partition_amount = domain_share_accumulated.shape
    head_width = partition_attention_maps.shape[1]
    tokens = domain_accumulated.reshape(row_count, partition_amount, head_width) / (
        domain_share_accumulated[:, :, None] + 1.0
    )
    queries = jnp.einsum("rmd,de->rme", tokens, partition_attention_maps[0])
    key_rows = jnp.einsum("rmd,de->rme", tokens, partition_attention_maps[1])
    values = jnp.einsum("rmd,de->rme", tokens, partition_attention_maps[2])
    scores = jnp.einsum("rme,rne->rmn", queries, key_rows) * head_width ** (-0.5)
    token_probs = jax.nn.softmax(scores, axis=-1)
    blended = jnp.einsum("rmn,rne->rme", token_probs, values)
    return blended.reshape(row_count, partition_amount * head_width).astype(jnp.bfloat16)


def spread_phase(
    tile_sequence, vertex_tallies, domain_sequence, partition_shares, tokens, readout_matrix
):
    tile_amount, tile_height, model_width = tile_sequence.shape
    attention_group_amount = tokens.shape[0] // MESHES
    partition_amount = partition_shares.shape[2] // attention_group_amount
    head_width = model_width // attention_group_amount
    tables = tokens.reshape(MESHES, attention_group_amount, partition_amount, head_width)
    chosen = jnp.take(tables, jnp.minimum(domain_sequence, MESHES - 1), axis=0)
    blended = jnp.einsum(
        "bphm,bhmd->bphd",
        partition_shares.reshape(
            tile_amount, tile_height, attention_group_amount, partition_amount
        ),
        chosen,
        preferred_element_type=jnp.float32,
    ).astype(jnp.bfloat16)
    projected = jnp.dot(
        blended.reshape(-1, model_width), readout_matrix, preferred_element_type=jnp.float32
    )
    living = (
        lax.broadcasted_iota(jnp.int32, (tile_amount, tile_height), 1) < vertex_tallies[:, None]
    ).astype(jnp.float32)
    result = (
        tile_sequence.reshape(-1, model_width).astype(jnp.float32) + projected
    ) * living.reshape(-1, 1)
    return result.reshape(tile_amount, tile_height, model_width).astype(jnp.bfloat16)


def on_device(
    vertex_values,
    position_domain_label,
    position_vertex_tally,
    normalizer_gain,
    embedding_matrix,
    partition_input_matrix,
    partition_score_matrix,
    softmax_sharpness,
    partition_attention_maps,
    readout_matrix,
):
    slot_total, tile_height, model_width = vertex_values.shape
    attention_group_amount = softmax_sharpness.shape[0]
    partition_amount = partition_score_matrix.shape[1]
    group_count = slot_total // 16
    grouped = (
        vertex_values.reshape(group_count, 16, tile_height, model_width),
        position_vertex_tally.reshape(group_count, 16),
        position_domain_label.reshape(group_count, 16),
    )

    def gather_step(running, lookup_element):
        partition_shares, domain_accumulated, domain_share_accumulated = partition_routine(
            lookup_element[0],
            lookup_element[1],
            lookup_element[2],
            normalizer_gain,
            embedding_matrix,
            partition_input_matrix,
            partition_score_matrix,
            softmax_sharpness,
        )
        return (
            (running[0] + domain_accumulated, running[1] + domain_share_accumulated),
            partition_shares,
        )

    initial = (
        jnp.zeros((MESHES, model_width * partition_amount), jnp.float32),
        jnp.zeros((MESHES, attention_group_amount * partition_amount), jnp.float32),
    )
    (domain_accumulated, domain_share_accumulated), partition_shares = lax.scan(
        gather_step, initial, grouped
    )
    whole_sums, whole_totals = lax.psum(
        (
            domain_accumulated.reshape(MESHES * attention_group_amount, -1),
            domain_share_accumulated.reshape(MESHES * attention_group_amount, -1),
        ),
        ("grp", "dev"),
    )
    tokens = attend_tokens(whole_sums, whole_totals, partition_attention_maps)

    def spread_step(lookup_element):
        return spread_phase(
            lookup_element[0],
            lookup_element[1],
            lookup_element[2],
            lookup_element[3],
            tokens,
            readout_matrix,
        )

    return lax.map(spread_step, grouped + (partition_shares,)).reshape(vertex_values.shape)


def solution(mesh):
    return jax.shard_map(
        on_device,
        mesh=mesh,
        in_specs=(
            P(("grp", "dev"), None, None),
            P(("grp", "dev")),
            P(("grp", "dev")),
            P(),
            P(),
            P(),
            P(),
            P(),
            P(),
            P(),
        ),
        out_specs=P(("grp", "dev"), None, None),
        check_vma=False,
    )
```

profile of v0, /device:TPU:1, one launch (start us, length us, event | category | flops | bytes accessed | tf_op | source)
XLA Modules:
  0.0 490.3 jit_solution(10821527517631763876)
XLA Ops:
  8.0 115.3 %while.26 = (s32[]{:T(128)}, f32[64,16384]{1,0:T(8,128)}, f32[64,512]{1,0:T(8,128)S(1)}, bf16[4,16,128,512]{2,3,1,0:T(8,128)(2,1)}, s32[4,16]{1,0:T(4,128)S(1)},...) while((s32[]{:T(128)}, f32[64,16384]{1,0:T(8,128)}, ...), condition=%wide.region_6.7_spmd.clone, body=%wide.region_0.6_spmd.clone.sunk | while | flops 723058752 | bytes 48028012 | solution.py:153
  57.7 5.0 %convolution_add_fusion.5 = f32[64,16384]{1,0:T(8,128)} fusion(bf16[16,16384]{1,0:T(8,128)(2,1)S(1)} %reshape.222, f32[64,16384]{1,0:T(8,128)} %get-tuple-element.383, pred[]{:T(512)S(6)} %compare.3, s32[16]{0:T(128)S(1)} %get-tuple-element.366), kind=kOutput, calls=%fused_computation.27.clone.1 | convolution fusion | flops 35652608 | bytes 8912961 | tf_op jit(solution)/shard_map/while/body/eval_jaxpr/dot_general | solution.py:56
  87.0 5.0 %convolution_add_fusion.5 = f32[64,16384]{1,0:T(8,128)} fusion(bf16[16,16384]{1,0:T(8,128)(2,1)S(1)} %reshape.222, f32[64,16384]{1,0:T(8,128)} %get-tuple-element.383, pred[]{:T(512)S(6)} %compare.3, s32[16]{0:T(128)S(1)} %get-tuple-element.366), kind=kOutput, calls=%fused_computation.27.clone.1 | convolution fusion | flops 35652608 | bytes 8912961 | tf_op jit(solution)/shard_map/while/body/eval_jaxpr/dot_general | solution.py:56
  116.4 5.0 %convolution_add_fusion.5 = f32[64,16384]{1,0:T(8,128)} fusion(bf16[16,16384]{1,0:T(8,128)(2,1)S(1)} %reshape.222, f32[64,16384]{1,0:T(8,128)} %get-tuple-element.383, pred[]{:T(512)S(6)} %compare.3, s32[16]{0:T(128)S(1)} %get-tuple-element.366), kind=kOutput, calls=%fused_computation.27.clone.1 | convolution fusion | flops 35652608 | bytes 8912961 | tf_op jit(solution)/shard_map/while/body/eval_jaxpr/dot_general | solution.py:56
  123.3 5.0 %reshape.192 = f32[512,2048]{1,0:T(8,128)} reshape(f32[64,16384]{1,0:T(8,128)} %get-tuple-element.111) | data formatting | bytes 8388608 | tf_op jit(solution)/shard_map/reshape | solution.py:158
  129.2 157.6 %all-reduce.3.cloned.1.call-done = (f32[512,2048]{1,0:T(8,128)}, f32[512,64]{0,1:T(8,128)}) async-done(((f32[512,2048]{1,0:T(8,128)}, f32[512,64]{0,1:T(8,128)}), (f32[512,2048]{1,0:T(8,128)}, f32[512,64]{0,1:T(8,128)})) %all-reduce.3.cloned.1.call-update) | async-done | bytes 4325392 | tf_op jit(solution)/shard_map/psum | solution.py:156
  290.3 5.4 %copy.52 = f32[512,2048]{1,0:T(8,128)} copy(f32[512,2048]{0,1:T(8,128)} %bitcast.167) | data formatting | bytes 8388608 | tf_op jit(solution)/shard_map/div | solution.py:70
  295.7 5.7 %div.49 = bf16[512,2048]{1,0:T(8,128)(2,1)} divide(f32[512,2048]{1,0:T(8,128)} %get-tuple-element.218, f32[512,2048]{1,0:T(8,128)} %copy.52) | non-fusion elementwise | flops 1048576 | bytes 10485760 | tf_op jit(solution)/shard_map/div | solution.py:70
  310.6 8.8 %copy.56 = bf16[512,64,32]{1,2,0:T(8,128)(2,1)} copy(bf16[512,64,32]{0,2,1:T(8,128)(2,1)} %fusion.39) | data formatting | bytes 4194304 | tf_op jit(solution)/shard_map/rmd,de->rme/dot_general | solution.py:73
  319.3 8.9 %copy.57 = bf16[512,64,32]{1,2,0:T(8,128)(2,1)} copy(bf16[512,64,32]{0,2,1:T(8,128)(2,1)} %fusion.37) | data formatting | bytes 4194304 | tf_op jit(solution)/shard_map/rmd,de->rme/dot_general | solution.py:74
  328.3 7.9 %copy.60 = bf16[512,64,32]{1,2,0:T(8,128)(2,1)} copy(bf16[512,64,32]{0,2,1:T(8,128)(2,1)S(1)} %copy-done) | data formatting | bytes 4194304 | tf_op jit(solution)/shard_map/rmd,de->rme/dot_general | solution.py:75
  336.1 12.5 %multiply_reduce_fusion.1 = (f32[512,64]{1,0:T(8,128)S(1)}, f32[512,64,64]{1,2,0:T(8,128)}) fusion(bf16[512,64,32]{1,2,0:T(8,128)(2,1)} %copy.56, bf16[512,64,32]{1,2,0:T(8,128)(2,1)} %copy.57), kind=kOutput, calls=%fused_computation.61 | convolution fusion | flops 138379264 | bytes 12713984 | tf_op jit(solution)/shard_map/rme,rne->rmn/dot_general | solution.py:76
  348.7 10.3 %fusion.28 = f32[512,64]{1,0:T(8,128)S(1)} fusion(f32[512,64,64]{1,2,0:T(8,128)} %get-tuple-element.229, f32[512,64]{1,0:T(8,128)S(1)} %get-tuple-element.228), kind=kLoop, calls=%fused_computation.62 | loop fusion | flops 6258688 | bytes 8650752 | tf_op jit(solution)/shard_map/reduce_sum | solution.py:77
  359.0 10.4 %fusion.32 = bf16[512,64,32]{1,2,0:T(8,128)(2,1)} fusion(bf16[512,64,32]{1,2,0:T(8,128)(2,1)} %copy.60, f32[512,64,64]{1,2,0:T(8,128)} %get-tuple-element.229, f32[512,64]{1,0:T(8,128)S(1)} %fusion.28, f32[512,64]{1,0:T(8,128)S(1)} %get-tuple-element.228), kind=kOutput, calls=%fused_computation.66 | convolution fusion | flops 140509184 | bytes 12845056 | tf_op jit(solution)/shard_map/rmn,rne->rme/dot_general | solution.py:78
  369.4 6.9 %copy.61 = bf16[512,64,32]{0,2,1:T(8,128)(2,1)} copy(bf16[512,64,32]{1,2,0:T(8,128)(2,1)} %fusion.32) | data formatting | bytes 4194304 | tf_op jit(solution)/shard_map/convert_element_type | solution.py:79
  379.3 104.2 %while.25 = (s32[]{:T(128)}, bf16[4,16,128,256]{3,2,1,0:T(8,128)(2,1)}, bf16[4,16,128,256]{3,2,1,0:T(8,128)(2,1)}, s32[4,16]{1,0:T(4,128)S(1)}, bf16[512,2048]{1...) while((s32[]{:T(128)}, ...), condition=%wide.region_12.13_spmd, body=%wide.region_11.12_spmd.sunk | while | flops 338433216 | bytes 26891408 | solution.py:175
  379.6 8.0 %reshape.221 = bf16[64,8,64,32]{3,2,1,0:T(8,128)(2,1)} reshape(bf16[512,2048]{1,0:T(8,128)(2,1)S(1)} %get-tuple-element.432) | data formatting | bytes 4194304 | tf_op jit(solution)/shard_map/while/body/eval_jaxpr/reshape | solution.py:89
  387.6 8.6 %copy.92 = bf16[64,8,64,32]{2,3,1,0:T(8,128)(2,1)} copy(bf16[64,8,64,32]{3,2,1,0:T(8,128)(2,1)} %reshape.221) | data formatting | bytes 4194304 | tf_op jit(solution)/shard_map/while/body/eval_jaxpr/reshape | solution.py:89
  405.6 8.0 %reshape.221 = bf16[64,8,64,32]{3,2,1,0:T(8,128)(2,1)} reshape(bf16[512,2048]{1,0:T(8,128)(2,1)S(1)} %get-tuple-element.432) | data formatting | bytes 4194304 | tf_op jit(solution)/shard_map/while/body/eval_jaxpr/reshape | solution.py:89
  413.6 8.6 %copy.92 = bf16[64,8,64,32]{2,3,1,0:T(8,128)(2,1)} copy(bf16[64,8,64,32]{3,2,1,0:T(8,128)(2,1)} %reshape.221) | data formatting | bytes 4194304 | tf_op jit(solution)/shard_map/while/body/eval_jaxpr/reshape | solution.py:89
  431.5 8.0 %reshape.221 = bf16[64,8,64,32]{3,2,1,0:T(8,128)(2,1)} reshape(bf16[512,2048]{1,0:T(8,128)(2,1)S(1)} %get-tuple-element.432) | data formatting | bytes 4194304 | tf_op jit(solution)/shard_map/while/body/eval_jaxpr/reshape | solution.py:89
  439.6 8.6 %copy.92 = bf16[64,8,64,32]{2,3,1,0:T(8,128)(2,1)} copy(bf16[64,8,64,32]{3,2,1,0:T(8,128)(2,1)} %reshape.221) | data formatting | bytes 4194304 | tf_op jit(solution)/shard_map/while/body/eval_jaxpr/reshape | solution.py:89
  457.5 8.0 %reshape.221 = bf16[64,8,64,32]{3,2,1,0:T(8,128)(2,1)} reshape(bf16[512,2048]{1,0:T(8,128)(2,1)S(1)} %get-tuple-element.432) | data formatting | bytes 4194304 | tf_op jit(solution)/shard_map/while/body/eval_jaxpr/reshape | solution.py:89
  465.6 8.6 %copy.92 = bf16[64,8,64,32]{2,3,1,0:T(8,128)(2,1)} copy(bf16[64,8,64,32]{3,2,1,0:T(8,128)(2,1)} %reshape.221) | data formatting | bytes 4194304 | tf_op jit(solution)/shard_map/while/body/eval_jaxpr/reshape | solution.py:89
  (184 shorter events, 154.7 us)
Async XLA Ops:
  6.5 280.3 %all-reduce.3.cloned.1.call-start = ((), (), s32[]{:S(2)}) async-start(), calls=%async_computation | async-start | bytes 8650752 | tf_op jit(solution)/shard_map/psum | solution.py:156
  8.0 5.3 %copy-start.1 = (bf16[256,256]{1,0:T(8,128)(2,1)S(1)}, bf16[256,256]{1,0:T(8,128)(2,1)}, u32[]{:S(2)}) copy-start(bf16[256,256]{1,0:T(8,128)(2,1)} %get-tuple-element.403) | copy-start | bytes 393220 | tf_op jit(solution)/shard_map/while
  11.5 3.1 copy-start.5
  11.5 3.1 copy-start.6
  18.3 3.5 copy-start.2
  35.2 5.3 %copy-start.1 = (bf16[256,256]{1,0:T(8,128)(2,1)S(1)}, bf16[256,256]{1,0:T(8,128)(2,1)}, u32[]{:S(2)}) copy-start(bf16[256,256]{1,0:T(8,128)(2,1)} %get-tuple-element.403) | copy-start | bytes 393220 | tf_op jit(solution)/shard_map/while
  38.8 3.1 copy-start.5
  38.8 3.1 copy-start.6
  45.5 3.5 copy-start.2
  64.6 5.3 %copy-start.1 = (bf16[256,256]{1,0:T(8,128)(2,1)S(1)}, bf16[256,256]{1,0:T(8,128)(2,1)}, u32[]{:S(2)}) copy-start(bf16[256,256]{1,0:T(8,128)(2,1)} %get-tuple-element.403) | copy-start | bytes 393220 | tf_op jit(solution)/shard_map/while
  68.1 3.1 copy-start.5
  68.1 3.1 copy-start.6
  74.8 3.5 copy-start.2
  94.0 5.3 %copy-start.1 = (bf16[256,256]{1,0:T(8,128)(2,1)S(1)}, bf16[256,256]{1,0:T(8,128)(2,1)}, u32[]{:S(2)}) copy-start(bf16[256,256]{1,0:T(8,128)(2,1)} %get-tuple-element.403) | copy-start | bytes 393220 | tf_op jit(solution)/shard_map/while
  97.5 3.1 copy-start.5
  97.5 3.1 copy-start.6
  104.2 3.5 copy-start.2
  301.3 3.1 copy-start.3
  319.3 8.9 %copy-start = (bf16[512,64,32]{0,2,1:T(8,128)(2,1)S(1)}, bf16[512,64,32]{0,2,1:T(8,128)(2,1)}, u32[]{:S(2)}) copy-start(bf16[512,64,32]{0,2,1:T(8,128)(2,1)} %fusion.35) | copy-start | bytes 6291460
  369.4 9.9 %copy-start.4 = (bf16[256,256]{1,0:T(8,128)(2,1)S(1)}, bf16[256,256]{1,0:T(8,128)(2,1)}, u32[]{:S(2)}) copy-start(bf16[256,256]{1,0:T(8,128)(2,1)} %param.23) | copy-start | bytes 393220
Sparse Core Ops, SparseCore 0:
  129.3 157.4 all-reduce.2
where the time goes:
time: 493 us; the launch traced here: 490 us
  local copies, waits for them, and re-layouts  182 us (37%)
  waiting for transfers between devices  158 us (32%)
  matrix products  84 us (17%)
  other arithmetic  52.1 us (11%)
  between operations  13.5 us (3%)
    psum x1, waiting for transfers between devices, on_device(): lax.psum((domain_accumulated.reshape(MESHES * attention_group_amount, -1)...  158 us
    reshape x8, local copies, waits for them, and re-layouts, spread_phase(): tokens.reshape(MESHES, attention_group_amount, partition_amount, head_width)  66.4 us
    dot_general x4, matrix products, partition_routine(): jnp.dot(one_hot.T, partial_sums.reshape(tile_amount, -1))  17.9 us
    sub x4, matrix products, partition_routine(): jax.nn.softmax(partition_scores, axis=-1) * living[:, :, None, None]  14.4 us
    reshape x4, local copies, waits for them, and re-layouts, partition_routine(): partial_sums.reshape(tile_amount, -1)  14 us
    reduce_sum x4, other arithmetic, partition_routine(): partial_totals = jnp.sum(partition_shares.astype(jnp.float32), axis=1)  13.5 us
    dot_general x1, matrix products, attend_tokens(): jnp.einsum('rme,rne->rmn', queries, key_rows) * head_width ** (-0.5)  12.5 us
    gather x4, local copies, waits for them, and re-layouts, spread_phase(): chosen = jnp.take(tables, jnp.minimum(domain_sequence, MESHES - 1), axis=0)  11.7 us
  transfers between devices with their start and end apart: 1, of which 1 were waited for; matrix products, arithmetic and copies ran while one was open for 0% of the time, Pallas kernels for 0%

commit v1 on v0

--- a/solution.py
+++ b/solution.py
@@ -154,11 +154,14 @@
         gather_step, initial, grouped
     )
     whole_sums, whole_totals = lax.psum(
-        (
-            domain_accumulated.reshape(MESHES * attention_group_amount, -1),
-            domain_share_accumulated.reshape(MESHES * attention_group_amount, -1),
+        lax.psum(
+            (
+                domain_accumulated.reshape(MESHES * attention_group_amount, -1),
+                domain_share_accumulated.reshape(MESHES * attention_group_amount, -1),
+            ),
+            "dev",
         ),
-        ("grp", "dev"),
+        "grp",
     )
     tokens = attend_tokens(whole_sums, whole_totals, partition_attention_maps)
 

time: 493 us -> 682 us (1.38)
  waiting for transfers between devices: 158 us -> 347 us
    psum x0 -> x1, waiting for transfers between devices: none -> 192 us  [on_device(): lax.psum(lax.psum((domain_accumulated.reshape(MESHES * attention_group_am...]
  transfers between devices with their start and end apart: 1 -> 2, of which waited for: 1 -> 2; matrix products, arithmetic and copies ran while one was open for 0% -> 0% of each run, Pallas kernels for 0% -> 0%
where the time goes in v1:
time: 682 us; the launch traced here: 679 us
  waiting for transfers between devices  347 us (51%)
  local copies, waits for them, and re-layouts  182 us (27%)
  matrix products  84 us (12%)
  other arithmetic  52.1 us (8%)
  between operations  13.5 us (2%)
    psum x1, waiting for transfers between devices, on_device(): lax.psum(lax.psum((domain_accumulated.reshape(MESHES * attention_group_am...  192 us
    psum x1, waiting for transfers between devices, on_device(): lax.psum((domain_accumulated.reshape(MESHES * attention_group_amount, -1)...  155 us
    reshape x8, local copies, waits for them, and re-layouts, spread_phase(): tokens.reshape(MESHES, attention_group_amount, partition_amount, head_width)  66.4 us
    dot_general x4, matrix products, partition_routine(): jnp.dot(one_hot.T, partial_sums.reshape(tile_amount, -1))  17.9 us
    sub x4, matrix products, partition_routine(): jax.nn.softmax(partition_scores, axis=-1) * living[:, :, None, None]  14.4 us
    reshape x4, local copies, waits for them, and re-layouts, partition_routine(): partial_sums.reshape(tile_amount, -1)  14 us
  transfers between devices with their start and end apart: 2, of which 2 were waited for; matrix products, arithmetic and copies ran while one was open for 0% of the time, Pallas kernels for 0%

profile of v1, /device:TPU:1, one launch (start us, length us, event | category | flops | bytes accessed | tf_op | source)
XLA Modules:
  0.0 679.4 jit_solution(11537528377936239577)
XLA Ops:
  8.0 115.3 %while.26 = (s32[]{:T(128)}, f32[64,16384]{1,0:T(8,128)}, f32[64,512]{1,0:T(8,128)S(1)}, bf16[4,16,128,512]{2,3,1,0:T(8,128)(2,1)}, s32[4,16]{1,0:T(4,128)S(1)},...) while((s32[]{:T(128)}, f32[64,16384]{1,0:T(8,128)}, ...), condition=%wide.region_6.7_spmd.clone, body=%wide.region_0.6_spmd.clone.sunk | while | flops 723058752 | bytes 48028012 | solution.py:153
  57.7 5.0 convolution_add_fusion.5
  87.0 5.0 convolution_add_fusion.5
  116.4 5.0 convolution_add_fusion.5
  129.4 154.9 %all-reduce.5.cloned.1.call-done = (f32[512,2048]{1,0:T(8,128)}, f32[512,64]{0,1:T(8,128)}) async-done(((f32[512,2048]{1,0:T(8,128)}, f32[512,64]{0,1:T(8,128)}), (f32[512,2048]{1,0:T(8,128)}, f32[512,64]{0,1:T(8,128)})) %all-reduce.5.cloned.1.call-update) | async-done | bytes 4325392 | tf_op jit(solution)/shard_map/psum | solution.py:157
  284.3 191.7 %all-reduce.7.cloned.1.call-done = (f32[512,2048]{1,0:T(8,128)}, f32[512,64]{0,1:T(8,128)}) async-done(((f32[512,2048]{1,0:T(8,128)}, f32[512,64]{0,1:T(8,128)}), (f32[512,2048]{1,0:T(8,128)}, f32[512,64]{0,1:T(8,128)})) %all-reduce.7.cloned.1.call-update) | async-done | bytes 4325392 | tf_op jit(solution)/shard_map/psum | solution.py:156
  479.5 5.4 copy.52
  484.9 5.7 div.49
  499.6 8.8 %copy.56 = bf16[512,64,32]{1,2,0:T(8,128)(2,1)} copy(bf16[512,64,32]{0,2,1:T(8,128)(2,1)} %fusion.39) | data formatting | bytes 4194304 | tf_op jit(solution)/shard_map/rmd,de->rme/dot_general | solution.py:73
  508.4 8.9 %copy.57 = bf16[512,64,32]{1,2,0:T(8,128)(2,1)} copy(bf16[512,64,32]{0,2,1:T(8,128)(2,1)} %fusion.37) | data formatting | bytes 4194304 | tf_op jit(solution)/shard_map/rmd,de->rme/dot_general | solution.py:74
  517.3 7.9 %copy.60 = bf16[512,64,32]{1,2,0:T(8,128)(2,1)} copy(bf16[512,64,32]{0,2,1:T(8,128)(2,1)S(1)} %copy-done) | data formatting | bytes 4194304 | tf_op jit(solution)/shard_map/rmd,de->rme/dot_general | solution.py:75
  525.2 12.5 %multiply_reduce_fusion.1 = (f32[512,64]{1,0:T(8,128)S(1)}, f32[512,64,64]{1,2,0:T(8,128)}) fusion(bf16[512,64,32]{1,2,0:T(8,128)(2,1)} %copy.56, bf16[512,64,32]{1,2,0:T(8,128)(2,1)} %copy.57), kind=kOutput, calls=%fused_computation.61 | convolution fusion | flops 138379264 | bytes 12713984 | tf_op jit(solution)/shard_map/rme,rne->rmn/dot_general | solution.py:76
  537.7 10.3 %fusion.28 = f32[512,64]{1,0:T(8,128)S(1)} fusion(f32[512,64,64]{1,2,0:T(8,128)} %get-tuple-element.231, f32[512,64]{1,0:T(8,128)S(1)} %get-tuple-element.230), kind=kLoop, calls=%fused_computation.62 | loop fusion | flops 6258688 | bytes 8650752 | tf_op jit(solution)/shard_map/reduce_sum | solution.py:77
  548.0 10.4 %fusion.32 = bf16[512,64,32]{1,2,0:T(8,128)(2,1)} fusion(bf16[512,64,32]{1,2,0:T(8,128)(2,1)} %copy.60, f32[512,64,64]{1,2,0:T(8,128)} %get-tuple-element.231, f32[512,64]{1,0:T(8,128)S(1)} %fusion.28, f32[512,64]{1,0:T(8,128)S(1)} %get-tuple-element.230), kind=kOutput, calls=%fused_computation.66 | convolution fusion | flops 140509184 | bytes 12845056 | tf_op jit(solution)/shard_map/rmn,rne->rme/dot_general | solution.py:78
  558.4 6.9 %copy.61 = bf16[512,64,32]{0,2,1:T(8,128)(2,1)} copy(bf16[512,64,32]{1,2,0:T(8,128)(2,1)} %fusion.32) | data formatting | bytes 4194304 | tf_op jit(solution)/shard_map/convert_element_type | solution.py:79
  568.3 104.2 %while.25 = (s32[]{:T(128)}, bf16[4,16,128,256]{3,2,1,0:T(8,128)(2,1)}, bf16[4,16,128,256]{3,2,1,0:T(8,128)(2,1)}, s32[4,16]{1,0:T(4,128)S(1)}, bf16[512,2048]{1...) while((s32[]{:T(128)}, ...), condition=%wide.region_14.15_spmd, body=%wide.region_13.14_spmd.sunk | while | flops 338433216 | bytes 26891408 | solution.py:178
  568.6 8.0 %reshape.221 = bf16[64,8,64,32]{3,2,1,0:T(8,128)(2,1)} reshape(bf16[512,2048]{1,0:T(8,128)(2,1)S(1)} %get-tuple-element.434) | data formatting | bytes 4194304 | tf_op jit(solution)/shard_map/while/body/eval_jaxpr/reshape | solution.py:89
  576.7 8.6 %copy.92 = bf16[64,8,64,32]{2,3,1,0:T(8,128)(2,1)} copy(bf16[64,8,64,32]{3,2,1,0:T(8,128)(2,1)} %reshape.221) | data formatting | bytes 4194304 | tf_op jit(solution)/shard_map/while/body/eval_jaxpr/reshape | solution.py:89
  594.6 8.0 %reshape.221 = bf16[64,8,64,32]{3,2,1,0:T(8,128)(2,1)} reshape(bf16[512,2048]{1,0:T(8,128)(2,1)S(1)} %get-tuple-element.434) | data formatting | bytes 4194304 | tf_op jit(solution)/shard_map/while/body/eval_jaxpr/reshape | solution.py:89
  602.6 8.6 %copy.92 = bf16[64,8,64,32]{2,3,1,0:T(8,128)(2,1)} copy(bf16[64,8,64,32]{3,2,1,0:T(8,128)(2,1)} %reshape.221) | data formatting | bytes 4194304 | tf_op jit(solution)/shard_map/while/body/eval_jaxpr/reshape | solution.py:89
  620.6 8.0 %reshape.221 = bf16[64,8,64,32]{3,2,1,0:T(8,128)(2,1)} reshape(bf16[512,2048]{1,0:T(8,128)(2,1)S(1)} %get-tuple-element.434) | data formatting | bytes 4194304 | tf_op jit(solution)/shard_map/while/body/eval_jaxpr/reshape | solution.py:89
  628.6 8.6 %copy.92 = bf16[64,8,64,32]{2,3,1,0:T(8,128)(2,1)} copy(bf16[64,8,64,32]{3,2,1,0:T(8,128)(2,1)} %reshape.221) | data formatting | bytes 4194304 | tf_op jit(solution)/shard_map/while/body/eval_jaxpr/reshape | solution.py:89
  646.6 8.0 %reshape.221 = bf16[64,8,64,32]{3,2,1,0:T(8,128)(2,1)} reshape(bf16[512,2048]{1,0:T(8,128)(2,1)S(1)} %get-tuple-element.434) | data formatting | bytes 4194304 | tf_op jit(solution)/shard_map/while/body/eval_jaxpr/reshape | solution.py:89
  654.6 8.6 %copy.92 = bf16[64,8,64,32]{2,3,1,0:T(8,128)(2,1)} copy(bf16[64,8,64,32]{3,2,1,0:T(8,128)(2,1)} %reshape.221) | data formatting | bytes 4194304 | tf_op jit(solution)/shard_map/while/body/eval_jaxpr/reshape | solution.py:89
  (187 shorter events, 159.8 us)
Async XLA Ops:
  6.5 277.8 %all-reduce.5.cloned.1.call-start = ((), (), s32[]{:S(2)}) async-start(), calls=%async_computation | async-start | bytes 8650752 | tf_op jit(solution)/shard_map/psum | solution.py:157
  8.0 5.3 copy-start.1
  11.5 3.1 copy-start.5
  11.5 3.1 copy-start.6
  18.3 3.5 copy-start.2
  35.2 5.3 copy-start.1
  38.8 3.1 copy-start.5
  38.8 3.1 copy-start.6
  45.5 3.5 copy-start.2
  64.6 5.3 copy-start.1
  68.1 3.1 copy-start.5
  68.1 3.1 copy-start.6
  74.8 3.5 copy-start.2
  93.9 5.3 copy-start.1
  97.5 3.1 copy-start.5
  97.5 3.1 copy-start.6
  104.2 3.5 copy-start.2
  129.2 346.9 %all-reduce.7.cloned.1.call-start = ((), (), s32[]{:S(2)}) async-start(), calls=%async_computation.1 | async-start | bytes 8650752 | tf_op jit(solution)/shard_map/psum | solution.py:156
  490.5 2.9 copy-start.3
  508.4 8.9 %copy-start = (bf16[512,64,32]{0,2,1:T(8,128)(2,1)S(1)}, bf16[512,64,32]{0,2,1:T(8,128)(2,1)}, u32[]{:S(2)}) copy-start(bf16[512,64,32]{0,2,1:T(8,128)(2,1)} %fusion.35) | copy-start | bytes 6291460
  558.4 9.9 %copy-start.4 = (bf16[256,256]{1,0:T(8,128)(2,1)S(1)}, bf16[256,256]{1,0:T(8,128)(2,1)}, u32[]{:S(2)}) copy-start(bf16[256,256]{1,0:T(8,128)(2,1)} %param.23) | copy-start | bytes 393220
Sparse Core Ops, SparseCore 0:
  129.3 154.9 all-reduce.4
  286.9 189.1 all-reduce.6
